TPU v7x, 32 devices: a whole 2x2x4 slice. The times are simulated.
32 devices in a mesh: farcp: 4 (over z), nearcp: 4 (over y, x), tp: 2 (over core).
Axes of the slice: x: 2, y: 2, z: 4, core: 2. Of those that a mesh axis runs over, the one named last changes fastest.
Arguments:
- raw_keys: bfloat16 [16, 8192, 8, 128], P(None, ('farcp', 'nearcp'), 'tp'), may hold values from -6 to 6
- raw_values: bfloat16 [16, 8192, 8, 128], P(None, ('farcp', 'nearcp'), 'tp'), may hold values from -6 to 6
- turn_angle: float32 [8192, 64], replicated, may hold values from -3.140625 to 3.140625
Outputs:
- stored_keys: bfloat16 [16, 8192, 8, 128], P(('farcp', 'nearcp'), None, 'tp')
- stored_values: bfloat16 [16, 8192, 8, 128], P(('farcp', 'nearcp'), None, 'tp')
- key_scale: float32 [16, 8, 128], P(('farcp', 'nearcp'), 'tp')
All inputs are finite; a program needn't handle non-finite values. Where the computation divides by a largest or mean magnitude, that divisor is 1e-20 or more.
Results may differ from a plain program's by a relative error of at most 0.001.
Values may be sent and summed in bfloat16 or wider, within the bound.
A program may use at most 128 MiB of HBM per device.

v0:
```python
import jax
import jax.numpy as jnp
from jax import lax
from jax.sharding import PartitionSpec as P


def turn_pairs(vectors, angle):
    half = vectors.shape[-1] // 2
    cosine, sine = (jnp.cos(angle)[None, :, None, :], jnp.sin(angle)[None, :, None, :])
    first, second = (vectors[..., :half], vectors[..., half:])
    return jnp.concatenate(
        [first * cosine - second * sine, second * cosine + first * sine], axis=-1
    )


def ready_to_store(plain_keys, angle):
    wide_keys = plain_keys.astype(jnp.float32)
    return turn_pairs(wide_keys, angle)


def body(raw_keys, raw_values, turn_angle):
    moved_keys, stored_values = (
        lax.all_to_all(raw_keys, ("farcp", "nearcp"), split_axis=0, concat_axis=1, tiled=True),
        lax.all_to_all(raw_values, ("farcp", "nearcp"), split_axis=0, concat_axis=1, tiled=True),
    )
    turned_keys = ready_to_store(moved_keys, turn_angle)
    key_scale = jnp.max(jnp.abs(turned_keys), axis=1)
    narrow_keys = (turned_keys / key_scale[:, None]).astype(jnp.bfloat16)
    return (narrow_keys, stored_values, key_scale)


def solution(mesh):
    placed = (
        P(None, ("farcp", "nearcp"), "tp", None),
        P(None, ("farcp", "nearcp"), "tp", None),
        P(),
    )
    return jax.shard_map(
        body,
        mesh=mesh,
        in_specs=placed,
        out_specs=(
            P(("farcp", "nearcp"), None, "tp", None),
            P(("farcp", "nearcp"), None, "tp", None),
            P(("farcp", "nearcp"), "tp", None),
        ),
        check_vma=False,
    )
```

profile of v0, /device:TPU:28, one launch (start us, length us, event | category | flops | bytes accessed | tf_op | source)
XLA Modules:
  0.0 390.4 jit_solution(15981875329838903006)
XLA Ops:
  0.6 188.6 %all_to_all.21 = bf16[16,512,4,128]{3,2,1,0:T(4,128)(2,1)} all-to-all(bf16[16,512,4,128]{3,2,1,0:T(4,128)(2,1)} %param.3), channel_id=1, replica_groups=mesh['farcp'=4,'nearcp'=4,'tp'=2] {'farcp','nearcp'}, dimensions={0} | all-to-all | bytes 16777216 | tf_op jit(solution)/shard_map/all_to_all | solution.py:23
  189.2 6.7 %all-to-all-start.1 = ((bf16[16,512,4,128]{3,2,1,0:T(4,128)(2,1)}), bf16[16,512,4,128]{3,2,1,0:T(4,128)(2,1)}, u32[]{:S(2)}, u32[]{:S(2)}) async-start(bf16[16,512,4,128]{3,2,1,0:T(4,128)(2,1)} %param.4), calls=%async_computation.1 | async-start | bytes 16777216 | tf_op jit(solution)/shard_map/all_to_all | solution.py:24
  196.0 9.4 %fusion = (f32[8192,64]{0,1:T(8,128)}, f32[8192,64]{0,1:T(8,128)S(1)}) fusion(f32[8192,64]{0,1:T(8,128)} %param.5), kind=kLoop, calls=%fused_computation.6 | loop fusion | bytes 6291456 | tf_op jit(solution)/shard_map/cos | solution.py:9
  205.4 3.8 copy.6
  209.2 2.8 copy.7
  212.0 0.0 copy-start.2
  212.0 0.0 copy-start.3
  212.0 5.9 %bitcast_convert_fusion = f32[1,4096,8,128]{3,2,1,0:T(8,128)S(1)} fusion(bf16[1,4096,8,128]{3,2,1,0:T(8,128)(2,1)} %bitcast.9), kind=kLoop, calls=%fused_computation.5 | loop fusion | flops 4194304 | bytes 25165824 | tf_op jit(solution)/shard_map/convert_element_type | solution.py:17
  217.9 0.0 copy-done.2
  217.9 0.1 copy-done.3
  218.0 14.5 %multiply_subtract_fusion = (f32[1,8192,4,64]{3,2,1,0:T(4,128)}, f32[1,8192,4,64]{3,2,1,0:T(4,128)}) fusion(f32[1,8192,4,128]{3,2,1,0:T(4,128)S(1)} %bitcast.8, f32[8192,64]{1,0:T(8,128)S(1)} %copy-done.3, f32[8192,64]{1,0:T(8,128)S(1)} %copy-done.2), kind=kLoop, calls=%fused_computation.3 | loop fusion | flops 12582912 | bytes 37748736 | tf_op jit(solution)/shard_map/sub | solution.py:12
  232.4 0.0 copy-start
  232.4 0.0 copy-start.1
  232.4 19.4 %abs_reduce_fusion = f32[4,128]{1,0:T(4,128)S(1)} fusion(f32[1,8192,4,64]{3,2,1,0:T(4,128)} %get-tuple-element.4, f32[1,8192,4,64]{3,2,1,0:T(4,128)} %get-tuple-element.3), kind=kLoop, calls=%fused_computation.1 | loop fusion | flops 12582400 | bytes 16779264 | tf_op jit(solution)/shard_map/reduce_max | solution.py:27
  251.8 0.0 copy-done
  251.8 1.0 copy-done.1
  252.8 0.0 copy-start.4
  252.8 10.3 %divide_convert_fusion = bf16[1,8192,4,128]{3,2,1,0:T(4,128)(2,1)} fusion(f32[4,128]{1,0:T(4,128)S(1)} %abs_reduce_fusion, f32[1,8192,4,64]{3,2,1,0:T(4,128)S(1)} %copy-done.1, f32[1,8192,4,64]{3,2,1,0:T(4,128)S(1)} %copy-done), kind=kLoop, calls=%fused_computation.4 | loop fusion | flops 12582912 | bytes 25167872 | tf_op jit(solution)/shard_map/convert_element_type | solution.py:28
  263.0 0.0 copy-done.4
  263.0 119.3 %all-to-all-done.1 = bf16[16,512,4,128]{3,2,1,0:T(4,128)(2,1)} async-done(((bf16[16,512,4,128]{3,2,1,0:T(4,128)(2,1)}), bf16[16,512,4,128]{3,2,1,0:T(4,128)(2,1)}, u32[]{:S(2)}, u32[]{:S(2)}) %all-to-all-start.1) | async-done | bytes 8388640 | tf_op jit(solution)/shard_map/all_to_all | solution.py:24
  382.3 8.1 %copy.9 = bf16[1,8192,4,128]{3,2,1,0:T(4,128)(2,1)} copy(bf16[1,8192,4,128]{3,2,1,0:T(4,128)(2,1)} %bitcast.2) | data formatting | bytes 16777216
Async XLA Ops:
  189.2 193.1 %all-to-all-start.1 = ((bf16[16,512,4,128]{3,2,1,0:T(4,128)(2,1)}), bf16[16,512,4,128]{3,2,1,0:T(4,128)(2,1)}, u32[]{:S(2)}, u32[]{:S(2)}) async-start(bf16[16,512,4,128]{3,2,1,0:T(4,128)(2,1)} %param.4), calls=%async_computation.1 | async-start | bytes 16777216 | tf_op jit(solution)/shard_map/all_to_all | solution.py:24
  212.0 5.9 %copy-start.2 = (f32[8192,64]{1,0:T(8,128)S(1)}, f32[8192,64]{1,0:T(8,128)}, u32[]{:S(2)}) copy-start(f32[8192,64]{1,0:T(8,128)} %copy.6) | copy-start | bytes 6291460
  212.0 6.0 %copy-start.3 = (f32[8192,64]{1,0:T(8,128)S(1)}, f32[8192,64]{1,0:T(8,128)}, u32[]{:S(2)}) copy-start(f32[8192,64]{1,0:T(8,128)} %copy.7) | copy-start | bytes 6291460
  232.4 19.4 %copy-start = (f32[1,8192,4,64]{3,2,1,0:T(4,128)S(1)}, f32[1,8192,4,64]{3,2,1,0:T(4,128)}, u32[]{:S(2)}) copy-start(f32[1,8192,4,64]{3,2,1,0:T(4,128)} %get-tuple-element.3) | copy-start | bytes 25165828
  232.4 20.4 %copy-start.1 = (f32[1,8192,4,64]{3,2,1,0:T(4,128)S(1)}, f32[1,8192,4,64]{3,2,1,0:T(4,128)}, u32[]{:S(2)}) copy-start(f32[1,8192,4,64]{3,2,1,0:T(4,128)} %get-tuple-element.4) | copy-start | bytes 25165828
  252.8 10.3 %copy-start.4 = (f32[4,128]{1,0:T(4,128)}, f32[4,128]{1,0:T(4,128)S(1)}, u32[]{:S(2)}) copy-start(f32[4,128]{1,0:T(4,128)S(1)} %abs_reduce_fusion) | copy-start | bytes 6148
where the time goes:
time: 391 us; the launch traced here: 390 us
  blocking collectives  189 us (48%)
  waiting for transfers between devices  119 us (30%)
  other arithmetic  50 us (13%)
  local copies, waits for them, and re-layouts  25.1 us (6%)
  starting transfers between devices  6.73 us (2%)
    all_to_all x1, blocking collectives, body(): lax.all_to_all(raw_keys, ('farcp', 'nearcp'), split_axis=0, concat_axis=1...  189 us
    all_to_all x1, waiting for transfers between devices, body(): lax.all_to_all(raw_values, ('farcp', 'nearcp'), split_axis=0, concat_axis...  119 us
    reduce_max x1, other arithmetic, body(): key_scale = jnp.max(jnp.abs(turned_keys), axis=1)  19.4 us
    sub x1, other arithmetic, turn_pairs(): first * cosine - second * sine  14.5 us
    cos x2, local copies, waits for them, and re-layouts, turn_pairs(): jnp.cos(angle)[None, :, None, :]  13.3 us
    convert_element_type x1, other arithmetic, body(): narrow_keys = (turned_keys / key_scale[:, None]).astype(jnp.bfloat16)  10.3 us
    unnamed x11, local copies, waits for them, and re-layouts  9.08 us
  transfers between devices with their start and end apart: 1, of which 1 were waited for; matrix products, arithmetic and copies ran while one was open for 17% of the time, Pallas kernels for 0%

commit v1 on v0

v1 whole, which is shorter than its diff:
```python
import functools

import jax
import jax.numpy as jnp
from jax import lax
from jax.experimental import pallas as pl
from jax.experimental.pallas import tpu as pltpu
from jax.sharding import PartitionSpec as P

MESH = pl.DeviceIdType.MESH


def partner_of(near, j, count):
    if count & (count - 1) == 0:
        other, bit = near, 1
        while bit < count:
            if j & bit:
                digit = lax.rem(lax.div(near, bit), 2)
                other = other + bit * (1 - 2 * digit)
            bit *= 2
        return other
    return lax.rem(2 * count - near - j, count)


def slots(count):
    return {pair: i for i, pair in enumerate((e, s) for e in range(1, count) for s in range(1, e + 1))}


def exchange_kernel(nf, nn, heads, key_in, value_in, angle, key_done, value_out, scale_out, key_side, value_side,
                    key_hold, value_hold, key_out, turned, cosines, sines, angles, scale, near_send, near_recv,
                    far_send, far_recv, own_sem, angle_sem, done_sem, scale_sem):
    f, n = lax.axis_index("farcp"), lax.axis_index("nearcp")
    me = f * nn + n
    slot = slots(nf)
    ins, outs = (key_in, value_in), (key_out, value_out)
    sides, holds = (key_side, value_side), (key_hold, value_hold)
    partners = [partner_of(n, j, nn) for j in range(nn)]

    barrier = pltpu.get_barrier_semaphore()
    for j in range(1, nn):
        pl.semaphore_signal(barrier, inc=1, device_id={"nearcp": partners[j]}, device_id_type=MESH)
    for way in (1, -1):
        @pl.when((f + way >= 0) & (f + way < nf))
        def _(way=way):
            pl.semaphore_signal(barrier, inc=1, device_id={"farcp": f + way}, device_id_type=MESH)
    pl.semaphore_wait(barrier, nn - 1 + jnp.where(f > 0, 1, 0) + jnp.where(f < nf - 1, 1, 0))

    def near_copy(t, j, r):
        d = lax.rem(f + r, nf)
        dst = outs[t].at[me] if r == 0 else sides[t].at[j - 1, d]
        i = (t * (nn - 1) + j - 1) * nf + r
        return pltpu.make_async_remote_copy(
            src_ref=ins[t].at[d * nn + partners[j]], dst_ref=dst,
            send_sem=near_send.at[i], recv_sem=near_recv.at[i],
            device_id={"nearcp": partners[j]}, device_id_type=MESH)

    def near_arrival(t, j, r):
        d = lax.rem(f + r, nf)
        dst = outs[t].at[f * nn + partners[j]] if r == 0 else sides[t].at[j - 1, d]
        i = (t * (nn - 1) + j - 1) * nf + r
        return pltpu.make_async_remote_copy(
            src_ref=dst, dst_ref=dst,
            send_sem=near_send.at[i], recv_sem=near_recv.at[i],
            device_id={"nearcp": partners[j]}, device_id_type=MESH)

    def far_copy(t, way, e, s, j):
        origin = f - way * (s - 1)
        end = origin + way * e
        active = (origin >= 0) & (origin < nf) & (end >= 0) & (end < nf)
        w = 0 if way == 1 else 1
        if s > 1:
            src = holds[t].at[w, slot[e, s - 1], j]
        elif j == 0:
            src = ins[t].at[end * nn + n]
        else:
            src = sides[t].at[j - 1, end]
        dst = outs[t].at[origin * nn + partners[j]] if s == e else holds[t].at[w, slot[e, s], j]
        i = ((t * 2 + w) * len(slot) + slot[e, s]) * nn + j
        return active, lambda: pltpu.make_async_remote_copy(
            src_ref=src, dst_ref=dst, send_sem=far_send.at[i], recv_sem=far_recv.at[i],
            device_id={"farcp": f + way}, device_id_type=MESH)

    def far_arrival(t, way, e, s, j):
        origin = f - way * s
        end = origin + way * e
        active = (origin >= 0) & (origin < nf) & (end >= 0) & (end < nf)
        w = 0 if way == 1 else 1
        dst = outs[t].at[origin * nn + partners[j]] if s == e else holds[t].at[w, slot[e, s], j]
        i = ((t * 2 + w) * len(slot) + slot[e, s]) * nn + j
        return active, lambda: pltpu.make_async_remote_copy(
            src_ref=dst, dst_ref=dst, send_sem=far_send.at[i], recv_sem=far_recv.at[i],
            device_id={"farcp": f - way}, device_id_type=MESH)

    own = [pltpu.make_async_copy(ins[t].at[me], outs[t].at[me], own_sem.at[t]) for t in range(2)]

    def first_hops(t, j):
        for e in range(nf - 1, 0, -1):
            for way in (1, -1):
                active, copy = far_copy(t, way, e, 1, j)
                @pl.when(active)
                def _(copy=copy, e=e, way=way):
                    if j > 0:
                        near_arrival(t, j, e if way == 1 else nf - e).wait_recv()
                    copy().start()

    def later_hops(t, s):
        for j in range(nn):
            for e in range(nf - 1, s - 1, -1):
                for way in (1, -1):
                    active, copy = far_copy(t, way, e, s, j)
                    _, arrival = far_arrival(t, way, e, s - 1, j)
                    @pl.when(active)
                    def _(copy=copy, arrival=arrival):
                        arrival().wait_recv()
                        copy().start()

    def final_arrivals(t):
        own[t].wait()
        for j in range(1, nn):
            near_arrival(t, j, 0).wait_recv()
        for e in range(1, nf):
            for way in (1, -1):
                for j in range(nn):
                    active, arrival = far_arrival(t, way, e, e, j)
                    @pl.when(active)
                    def _(arrival=arrival):
                        arrival().wait_recv()

    def finish_keys():
        blocks, rows, size = key_out.shape
        half = size // 2
        length = rows // heads
        group = 8
        def turn(b, top):
            place = angles[:, pl.ds(pl.multiple_of(b * length, length), length)]
            cosine, sine = jnp.cos(place), jnp.sin(place)
            cosine = jnp.concatenate([cosine, cosine], axis=0).T
            sine = jnp.concatenate([-sine, sine], axis=0).T
            for h in range(heads):
                cosines[pl.ds(h, length, stride=heads), :] = cosine
                sines[pl.ds(h, length, stride=heads), :] = sine
            piece = min(256, rows)
            def part(i, top):
                at = pl.ds(pl.multiple_of(i * piece, piece), piece)
                wide = key_out[b, at, :].astype(jnp.float32)
                y = wide * cosines[at, :] + pltpu.roll(wide, half, 1) * sines[at, :]
                turned[b, at, :] = y
                return jnp.maximum(top, jnp.max(jnp.abs(y).reshape(piece // group, group, size), axis=0))
            return lax.fori_loop(0, rows // piece, part, top)
        top = lax.fori_loop(0, blocks, turn, jnp.zeros((group, size), jnp.float32))
        biggest = top[:heads]
        for at in range(heads, group, heads):
            biggest = jnp.maximum(biggest, top[at:at + heads])
        scale[...] = biggest
        spread = jnp.concatenate([biggest] * (group // heads), axis=0)
        def narrow(b, carry):
            piece = min(256, rows)
            def part(i, carry):
                at = pl.ds(pl.multiple_of(i * piece, piece), piece)
                y = turned[b, at, :].reshape(piece // group, group, size)
                key_out[b, at, :] = (y / spread[None]).reshape(piece, size).astype(key_out.dtype)
                return carry
            lax.fori_loop(0, rows // piece, part, 0)
            pltpu.make_async_copy(key_out.at[b], key_done.at[b], done_sem.at[b]).start()
            return carry
        lax.fori_loop(0, blocks, narrow, 0)
        pltpu.make_async_copy(scale, scale_out, scale_sem).start()

    angle_copy = pltpu.make_async_copy(angle, angles, angle_sem)
    first_hops(0, 0)
    for t in range(2):
        for j in range(1, nn):
            for r in list(range(1, nf)) + [0]:
                near_copy(t, j, r).start()
    first_hops(1, 0)
    for copy in own:
        copy.start()
    angle_copy.start()
    for j in range(1, nn):
        first_hops(0, j)
    for s in range(2, nf - 1):
        later_hops(0, s)
    for j in range(1, nn):
        first_hops(1, j)
    if nf > 2:
        later_hops(0, nf - 1)
    final_arrivals(0)
    angle_copy.wait()
    finish_keys()
    for s in range(2, nf):
        later_hops(1, s)
    final_arrivals(1)
    for t in range(2):
        for j in range(1, nn):
            for r in range(nf):
                near_copy(t, j, r).wait_send()
        for (e, s) in slot:
            for way in (1, -1):
                for j in range(nn):
                    active, copy = far_copy(t, way, e, s, j)
                    @pl.when(active)
                    def _(copy=copy):
                        copy().wait_send()
    for b in range(nf * nn):
        pltpu.make_async_copy(key_out.at[b], key_done.at[b], done_sem.at[b]).wait()
    pltpu.make_async_copy(scale, scale_out, scale_sem).wait()


def exchange(nf, nn, heads, keys, values, angle):
    block = keys.shape[1:]
    k = len(slots(nf))
    out = jax.ShapeDtypeStruct(keys.shape, keys.dtype)
    side = jax.ShapeDtypeStruct((nn - 1, nf) + block, keys.dtype)
    hold = jax.ShapeDtypeStruct((2, k, nn) + block, keys.dtype)
    top = jax.ShapeDtypeStruct((heads, block[-1]), jnp.float32)
    dma = pltpu.SemaphoreType.DMA
    return pl.pallas_call(
        functools.partial(exchange_kernel, nf, nn, heads),
        out_shape=[out, out, top, side, side, hold, hold],
        in_specs=[pl.BlockSpec(memory_space=pl.ANY)] * 3,
        out_specs=[pl.BlockSpec(memory_space=pl.ANY)] * 7,
        scratch_shapes=[pltpu.VMEM(keys.shape, keys.dtype), pltpu.VMEM(keys.shape, jnp.float32),
                        pltpu.VMEM(block, jnp.float32), pltpu.VMEM(block, jnp.float32),
                        pltpu.VMEM(angle.shape, angle.dtype), pltpu.VMEM(top.shape, jnp.float32),
                        dma((2 * (nn - 1) * nf,)), dma((2 * (nn - 1) * nf,)),
                        dma((4 * k * nn,)), dma((4 * k * nn,)), dma((2,)), dma, dma((nf * nn,)), dma],
        compiler_params=pltpu.CompilerParams(
            collective_id=0, has_side_effects=True, vmem_limit_bytes=40 * 1024 * 1024),
    )(keys, values, angle)[:3]


def solution(mesh):
    nf, nn = mesh.shape["farcp"], mesh.shape["nearcp"]

    def body(raw_keys, raw_values, turn_angle):
        batch, length, heads, size = raw_keys.shape
        assert batch == nf * nn and 8 % heads == 0
        flat = (batch, length * heads, size)
        keys, values, scale = exchange(
            nf, nn, heads, raw_keys.reshape(flat), raw_values.reshape(flat), turn_angle.T)
        moved = (1, nf * nn * length, heads, size)
        return keys.reshape(moved), values.reshape(moved), scale[None]

    placed = P(None, ("farcp", "nearcp"), "tp", None)
    moved = P(("farcp", "nearcp"), None, "tp", None)
    return jax.shard_map(
        body,
        mesh=mesh,
        in_specs=(placed, placed, P()),
        out_specs=(moved, moved, P(("farcp", "nearcp"), "tp", None)),
        check_vma=False,
    )
```

time: 391 us -> 385 us (0.985)
  Pallas kernels: 0 us -> 365 us
  blocking collectives: 189 us -> 0 us
  waiting for transfers between devices: 119 us -> 0 us
  other arithmetic: 50 us -> 0 us
  local copies, waits for them, and re-layouts: 25.1 us -> 14.6 us
  starting transfers between devices: 6.73 us -> 0 us
    pallas_call x0 -> x1, Pallas kernels: none -> 365 us  [exchange(): pl.pallas_call(functools.partial(exchange_kernel, nf, nn, heads), out_sha...]
    all_to_all x1 -> x0, blocking collectives: 189 us -> none  [body(): lax.all_to_all(raw_keys, ('farcp', 'nearcp'), split_axis=0, concat_axis=1...]
    all_to_all x1 -> x0, waiting for transfers between devices: 119 us -> none  [body(): lax.all_to_all(raw_values, ('farcp', 'nearcp'), split_axis=0, concat_axis...]
    reduce_max x1 -> x0, other arithmetic: 19.4 us -> none  [body(): key_scale = jnp.max(jnp.abs(turned_keys), axis=1)]
    convert_element_type x2 -> x0, other arithmetic: 16.2 us -> none  [the longest x1 10.3 us: body(): narrow_keys = (turned_keys / key_scale[:, None]).astype(jnp.bfloat16)]
    sub x1 -> x0, other arithmetic: 14.5 us -> none  [turn_pairs(): first * cosine - second * sine]
    cos x2 -> x0, local copies, waits for them, and re-layouts: 13.3 us -> none  [turn_pairs(): jnp.cos(angle)[None, :, None, :]]
    all_to_all x1 -> x0, starting transfers between devices: 6.73 us -> none  [body(): lax.all_to_all(raw_values, ('farcp', 'nearcp'), split_axis=0, concat_axis...]
  transfers between devices with their start and end apart: 1 -> 0, of which waited for: 1 -> 0; matrix products, arithmetic and copies ran while one was open for 17% -> 0% of each run, Pallas kernels for 0% -> 0%
where the time goes in v1:
time: 385 us; the launch traced here: 381 us
  Pallas kernels  365 us (95%)
  local copies, waits for them, and re-layouts  14.6 us (4%)
    pallas_call x1, Pallas kernels, exchange(): pl.pallas_call(functools.partial(exchange_kernel, nf, nn, heads), out_sha...  365 us
    unnamed x7, local copies, waits for them, and re-layouts  14.6 us

profile of v1, /device:TPU:28, one launch (start us, length us, event | category | flops | bytes accessed | tf_op | source)
XLA Modules:
  0.0 380.6 jit_solution(5339705971190944946)
XLA Ops:
  0.6 0.0 copy-start
  0.6 1.6 copy-done
  2.2 365.4 %shard_map.58 = (bf16[16,2048,128]{2,1,0:T(8,128)(2,1)}, bf16[16,2048,128]{2,1,0:T(8,128)(2,1)}, f32[4,128]{1,0:T(4,128)S(1)}, bf16[3,4,2048,128]{3,2,1,0:T(8,12...) custom-call(bf16[16,2048,128]{2,1,0:T(8,128)(2,1)} %bitcast.8, ...), custom_call_target="tpu_custom_call" | custom-call | tf_op jit(solution)/shard_map/pallas_call | solution.py:217
  367.6 0.0 copy-start.1
  367.6 9.1 %copy.9 = bf16[1,8192,4,128]{3,2,1,0:T(4,128)(2,1)} copy(bf16[1,8192,4,128]{3,2,1,0:T(4,128)(2,1)} %bitcast.11) | data formatting | bytes 16777216
  376.7 0.0 copy-done.1
  376.7 3.4 copy.10
  380.1 0.6 copy.11
Async XLA Ops:
  0.6 1.6 copy-start
  367.6 9.1 %copy-start.1 = (bf16[16,2048,128]{2,1,0:T(8,128)(2,1)S(1)}, bf16[16,2048,128]{2,1,0:T(8,128)(2,1)}, u32[]{:S(2)}) copy-start(bf16[16,2048,128]{2,1,0:T(8,128)(2,1)} %get-tuple-element.7) | copy-start | bytes 25165828
